TPU v7x, 256 devices: a whole 4x4x8 slice. The times are simulated.
256 devices in a mesh: dp: 8 (over z_lo, core), vocab: 32 (over z_hi, x, y).
Axes of the slice: x: 4, y: 4, z: 8 (z_hi: 2, z_lo: 4; z = z_hi * 4 + z_lo), core: 2. Of those that a mesh axis runs over, the one named last changes fastest.
Arguments:
- policy_hidden: bfloat16 [1024, 4096], P('dp'), may hold values from -84 to 84
- policy_weight: bfloat16 [4096, 65536], P('dp', 'vocab'), may hold values from -0.09375 to 0.09375
- reference_hidden: bfloat16 [1024, 4096], P(('dp', 'vocab')), may hold values from -84 to 84
- reference_weight: bfloat16 [4096, 65536], P(None, ('dp', 'vocab')), may hold values from -0.09375 to 0.09375
- targets: int32 [1024], replicated, may hold values from 0 to 65535
- response_mask: int32 [1024], replicated, may hold values 0 or 1
- pair_index: int32 [32], replicated, may hold values from 0 to 31, each once
Outputs:
- hidden_grad: bfloat16 [1024, 4096], P('vocab', 'dp')
- weight_grad: bfloat16 [4096, 65536], P('dp', 'vocab')
- total_loss: float32 [], replicated
Inputs may be any that keep to these rules, and one draw needn't show every extreme that they name: `pair_index`: each number of 0 to 31 once; entries 2p and 2p + 1 are the chosen and the rejected sequence of pair p.
All inputs are finite; a program needn't handle non-finite values.
Results may differ from a plain program's by a relative error of at most 0.005.
The roundings to bfloat16 on the way count: a program that leaves them out, or rounds other values in their place, can miss the bound.
Values may be sent and summed in bfloat16 or wider, within the bound.
A program may use at most 128 MiB of HBM per device.

v0:
```python
import jax
import jax.numpy as jnp
from jax import lax
from jax.sharding import Mesh
from jax.sharding import PartitionSpec as P

SEQ_LEN = 32
DP = ("dp_0", "dp_1")
VOCAB = ("vocab_0", "vocab_1", "vocab_2")
DP_VOCAB = ("dp_0", "dp_1", "vocab_0", "vocab_1", "vocab_2")
beta = 0.1
loss_scale = 4096.0


def all_in_one(value, axis):
    leaves = jax.tree.leaves(value)
    order = sorted(range(len(leaves)), key=lambda k: -leaves[k].size)
    width = (1, *leaves[order[0]].shape)[-1]
    lines = [
        jnp.pad(leaves[k].reshape(-1), (0, -leaves[k].size % width)).reshape(-1, width)
        for k in order
    ]
    both, at, found = (lax.all_gather(jnp.concatenate(lines), axis), 0, {})
    for k, line in zip(order, lines):
        slab = both[:, at : at + len(line)].reshape(len(both), -1)
        found[k] = slab[:, : leaves[k].size].reshape(-1, *leaves[k].shape)
        at += len(line)
    numbers = iter(range(len(leaves)))
    return jax.tree.map(lambda _: found[next(numbers)], value)


def merged_by_axis(value, axes, combine):
    for axis in axes:
        pieces = all_in_one(value, axis)
        value = jax.tree.map(lambda part: part[0], pieces)
        for k in range(1, lax.axis_size(axis)):
            value = combine(value, jax.tree.map(lambda part: part[k], pieces))
    return value


def in_blocks(value, dim, peers):
    shape = value.shape
    tiles = value.reshape(*shape[:dim], peers, shape[dim] // peers, *shape[dim + 1 :])
    return jnp.moveaxis(tiles, dim, 0)


def sum_at_owner(value, axis, dim):
    peers = lax.axis_size(axis)
    tiles = lax.all_to_all(in_blocks(value, dim, peers), axis, 0, 0, tiled=True)
    return jnp.sum(tiles, axis=0)


def pair_terms(log_ratio, pair_index):
    chosen = pair_index[0::2]
    rejected = pair_index[1::2]
    margin = beta * (log_ratio[chosen] - log_ratio[rejected])
    pair_count = chosen.shape[0]
    total_loss = jnp.sum(jax.nn.softplus(-margin)) / pair_count
    weight = -beta * loss_scale * jax.nn.sigmoid(-margin) / pair_count
    numbers = jnp.arange(log_ratio.shape[0], dtype=jnp.int32)[:, None]
    factor = jnp.sum(
        jnp.where(numbers == chosen[None, :], weight[None, :], 0.0)
        - jnp.where(numbers == rejected[None, :], weight[None, :], 0.0),
        axis=1,
    )
    return (total_loss, factor)


def local_pick(logits, targets, offset, axis):
    column_ids = lax.broadcasted_iota(jnp.int32, logits.shape, axis)
    shifted = targets - offset
    wanted = shifted[:, None] if axis == 1 else shifted[None, :]
    return jnp.sum(jnp.where(column_ids == wanted, logits, 0.0), axis=axis)


def merge_pair(earlier, later):
    largest = jnp.maximum(earlier[0], later[0])
    exp_total = earlier[1] * jnp.exp(earlier[0] - largest) + later[1] * jnp.exp(later[0] - largest)
    return (largest, exp_total, earlier[2] + later[2])


def merge_heads(earlier, later):
    return merge_pair(earlier[0:3], later[0:3]) + merge_pair(earlier[3:6], later[3:6])


def local(
    policy_hidden,
    policy_weight,
    reference_hidden,
    reference_weight,
    targets,
    response_mask,
    pair_index,
):
    data_index = lax.axis_index(DP)
    vocab_index = lax.axis_index(VOCAB)
    vocab_devices = lax.axis_size(VOCAB)
    data_devices = lax.axis_size(DP)
    policy_width = policy_weight.shape[1]
    reference_width = reference_weight.shape[1]
    active = response_mask.astype(jnp.float32)
    columns = lax.all_to_all(policy_hidden, DP, split_axis=1, concat_axis=0, tiled=True)
    reference_logits = jnp.dot(
        lax.all_gather(reference_hidden, DP_VOCAB, axis=0, tiled=True),
        reference_weight,
        preferred_element_type=jnp.float32,
    )
    reference_offset = (data_index * vocab_devices + vocab_index) * reference_width
    reference_top = jnp.max(reference_logits, axis=1)
    reference_pick = local_pick(reference_logits, targets, reference_offset, 1)
    slice_width = policy_width // data_devices
    weight_block = policy_weight
    policy_logits = lax.psum_scatter(
        lax.dot_general(
            weight_block, columns, (((0,), (1,)), ((), ())), preferred_element_type=jnp.float32
        ),
        DP,
        scatter_dimension=0,
        tiled=True,
    )
    policy_offset = vocab_index * policy_width + data_index * slice_width
    policy_top = jnp.max(policy_logits, axis=0)
    policy_pick = local_pick(policy_logits, targets, policy_offset, 0)
    local_stats = (
        policy_top,
        jnp.sum(jnp.exp(policy_logits - policy_top[None, :]), axis=0),
        policy_pick,
        reference_top,
        jnp.sum(jnp.exp(reference_logits - reference_top[:, None]), axis=1),
        reference_pick,
    )
    merged = merged_by_axis(local_stats, DP_VOCAB, merge_heads)
    policy_total = merged[0] + jnp.log(merged[1])
    reference_logp = merged[5] - merged[3] - jnp.log(merged[4])
    log_ratio = jnp.sum(
        (active * (merged[2] - policy_total - reference_logp)).reshape(-1, SEQ_LEN), axis=1
    )
    total_loss, factor = pair_terms(log_ratio, pair_index)
    token_scale = active * jnp.repeat(factor, SEQ_LEN)
    row_ids = lax.broadcasted_iota(jnp.int32, policy_logits.shape, 0)
    onehot = (row_ids == (targets - policy_offset)[None, :]).astype(jnp.float32)
    logit_grad = (
        token_scale[None, :] * (onehot - jnp.exp(policy_logits - policy_total[None, :]))
    ).astype(jnp.bfloat16)
    segment = lax.all_gather(logit_grad, DP, axis=0, tiled=True)
    weight_block = policy_weight
    column_grad = lax.dot_general(
        columns, segment, (((0,), (1,)), ((), ())), preferred_element_type=jnp.float32
    )
    hidden_part = lax.dot_general(
        segment, weight_block, (((0,), (1,)), ((), ())), preferred_element_type=jnp.float32
    )
    weight_grad, hidden_part = (column_grad, hidden_part)
    hidden_grad = sum_at_owner(hidden_part, VOCAB, 0)
    return (hidden_grad.astype(jnp.bfloat16), weight_grad.astype(jnp.bfloat16), total_loss)


def solution(mesh):
    torus = Mesh(
        mesh.devices.reshape(4, 2, 2, 4, 4), ("dp_0", "dp_1", "vocab_0", "vocab_1", "vocab_2")
    )
    in_specs = (P(DP, None), P(DP, VOCAB), P(DP_VOCAB, None), P(None, DP_VOCAB), P(), P(), P())
    out_specs = (P(VOCAB, DP), P(DP, VOCAB), P())
    return jax.shard_map(local, mesh=torus, in_specs=in_specs, out_specs=out_specs, check_vma=False)
```

profile of v0, /device:TPU:38, one launch (start us, length us, event | category | flops | bytes accessed | tf_op | source)
XLA Modules:
  0.0 990.6 jit_solution(14023371967877538093)
XLA Ops:
  8.1 0.7 all-gather.16.cloned.1.call-update
  8.8 2.3 copy.18
  11.1 30.3 %all_to_all.24 = bf16[128,8,512]{0,2,1:T(8,128)(2,1)S(1)} all-to-all(bf16[128,8,512]{0,2,1:T(8,128)(2,1)} %bitcast.453), channel_id=1, replica_groups=mesh['dp_0'=4,'dp_1'=2,'vocab_0'=2,'vocab_1'=4,'vocab_2'=4] {'dp_0','dp_1'}, dimensions={1} | all-to-all | bytes 2097152 | tf_op jit(solution)/shard_map/all_to_all | solution.py:102
  41.3 1.3 copy.19
  42.6 6.8 fusion.94
  49.6 0.6 copy-done.5
  50.1 0.1 slice.613
  50.2 0.1 slice.516
  50.4 675.5 %all-gather.16.cloned.1.call-done = bf16[256,4,4096]{2,1,0:T(4,128)(2,1)} async-done(((bf16[1,4,4096]{2,1,0:T(4,128)(2,1)}), bf16[256,4,4096]{2,1,0:T(4,128)(2,1)}) %all-gather.16.cloned.1.call-update) | async-done | bytes 8388624 | tf_op jit(solution)/shard_map/all_gather | solution.py:104
  725.9 12.5 %reshape.1600 = bf16[1024,4096]{1,0:T(8,128)(2,1)} reshape(bf16[256,4,4096]{2,1,0:T(4,128)(2,1)} %all-gather.16.cloned.1.call-done) | data formatting | bytes 16777216
  738.4 6.4 fusion.93
  744.8 0.3 select_reduce_fusion
  745.1 1.3 reduce_max.18
  746.4 1.6 select_reduce_fusion.1
  748.1 59.3 %all-gather.6 = f32[4,6,1024]{2,1,0:T(8,128)S(1)} all-gather(f32[1,6,1024]{2,1,0:T(8,128)S(1)} %bitcast.457), channel_id=2, replica_groups=mesh['dp_0'=4,'dp_1'=2,'vocab_0'=2,'vocab_1'=4,'vocab_2'=4] {'dp_0'}, dimensions={0}, use_global_device_ids=true | all-gather | bytes 122880 | tf_op jit(solution)/shard_map/all_gather | solution.py:23
  807.6 1.9 all-gather.7
  809.5 8.5 all-gather.8
  818.1 21.7 %all-gather.9 = f32[4,6,1024]{2,1,0:T(8,128)S(1)} all-gather(f32[1,6,1024]{2,1,0:T(8,128)S(1)} %bitcast.460), channel_id=5, replica_groups=mesh['dp_0'=4,'dp_1'=2,'vocab_0'=2,'vocab_1'=4,'vocab_2'=4] {'vocab_1'}, dimensions={0}, use_global_device_ids=true | all-gather | bytes 122880 | tf_op jit(solution)/shard_map/all_gather | solution.py:23
  839.9 0.1 fusion.3
  840.0 12.1 %all-gather.10 = f32[4,6,1024]{2,1,0:T(8,128)S(1)} all-gather(f32[1,6,1024]{2,1,0:T(8,128)S(1)} %bitcast.461), channel_id=6, replica_groups=mesh['dp_0'=4,'dp_1'=2,'vocab_0'=2,'vocab_1'=4,'vocab_2'=4] {'vocab_2'}, dimensions={0}, use_global_device_ids=true | all-gather | bytes 122880 | tf_op jit(solution)/shard_map/all_gather | solution.py:23
  852.3 0.1 reduce_sum.76
  852.4 0.7 gather_fusion.1
  853.1 0.7 gather_fusion
  853.8 0.6 fusion.83
  854.6 1.1 multiply_convert_fusion
  855.7 50.3 %all-gather.14.cloned.1.call-done = bf16[2048,1024]{1,0:T(8,128)(2,1)} async-done(((bf16[256,1024]{1,0:T(8,128)(2,1)}), bf16[2048,1024]{1,0:T(8,128)(2,1)}) %all-gather.14.cloned.1.call-update) | async-done | bytes 4194320 | tf_op jit(solution)/shard_map/all_gather | solution.py:145
  906.1 5.9 fusion.95
  912.0 13.1 %all-to-all-start.1 = ((f32[32,32,512]{2,1,0:T(8,128)}), f32[32,32,512]{2,1,0:T(8,128)}, u32[]{:S(2)}, u32[]{:S(2)}) async-start(f32[32,32,512]{2,1,0:T(8,128)} %bitcast.454), calls=%async_computation.2 | async-start | bytes 4194304 | tf_op jit(solution)/shard_map/all_to_all | solution.py:49
  925.8 5.9 fusion
  931.7 3.9 copy.20
  935.6 44.1 %all-to-all-done.1 = f32[32,32,512]{2,1,0:T(8,128)} async-done(((f32[32,32,512]{2,1,0:T(8,128)}), f32[32,32,512]{2,1,0:T(8,128)}, u32[]{:S(2)}, u32[]{:S(2)}) %all-to-all-start.1) | async-done | bytes 2097184 | tf_op jit(solution)/shard_map/all_to_all | solution.py:49
  979.7 2.4 reduce_sum.78
  (42 shorter events, 1.2 us)
Async XLA Ops:
  8.0 34.6 %copy-start = (bf16[512,2048]{1,0:T(8,128)(2,1)S(1)}, bf16[512,2048]{1,0:T(8,128)(2,1)}, u32[]{:S(2)}) copy-start(bf16[512,2048]{1,0:T(8,128)(2,1)} %param.8) | copy-start | bytes 6291460
  8.0 717.9 %all-gather.16.cloned.1.call-start = ((), (), s32[]{:S(2)}) async-start(), calls=%async_computation.5 | async-start | bytes 8421376 | tf_op jit(solution)/shard_map/all_gather | solution.py:104
  8.7 736.4 %reduce-scatter.2.cloned.1.call-start = ((), (), s32[]{:S(2)}) async-start(), calls=%async_computation.3 | async-start | bytes 9437184 | tf_op jit(solution)/shard_map/reduce_scatter | solution.py:113
  49.5 0.7 copy-start.5
  49.5 0.9 copy-start.4
  49.5 856.6 %all-gather.14.cloned.1.call-start = ((), (), s32[]{:S(2)}) async-start(), calls=%async_computation.4 | async-start | bytes 4718592 | tf_op jit(solution)/shard_map/all_gather | solution.py:145
  745.1 107.1 %copy-start.3 = (s32[1024]{0:T(1024)S(1)}, s32[1024]{0:T(1024)}, u32[]{:S(2)}) copy-start(s32[1024]{0:T(1024)} %param.12) | copy-start | bytes 12292
  746.4 108.2 %copy-start.1 = (f32[256,1024]{1,0:T(8,128)S(1)}, f32[256,1024]{1,0:T(8,128)}, u32[]{:S(2)}) copy-start(f32[256,1024]{1,0:T(8,128)} %reduce-scatter.2.cloned.1.call-done) | copy-start | bytes 3145732
  912.0 13.8 %copy-start.2 = (bf16[8,128,512]{2,1,0:T(8,128)(2,1)S(1)}, bf16[8,128,512]{2,1,0:T(8,128)(2,1)}, u32[]{:S(2)}) copy-start(bf16[8,128,512]{2,1,0:T(8,128)(2,1)} %copy.19) | copy-start | bytes 3145732
  912.0 67.7 %all-to-all-start.1 = ((f32[32,32,512]{2,1,0:T(8,128)}), f32[32,32,512]{2,1,0:T(8,128)}, u32[]{:S(2)}, u32[]{:S(2)}) async-start(f32[32,32,512]{2,1,0:T(8,128)} %bitcast.454), calls=%async_computation.2 | async-start | bytes 4194304 | tf_op jit(solution)/shard_map/all_to_all | solution.py:49
Sparse Core Ops, SparseCore 0:
  10.7 715.1 all-gather.15
Sparse Core Ops, SparseCore 1:
  49.6 93.9 reduce-scatter.1
  855.8 50.2 all-gather.13
where the time goes:
time: 991 us
  waiting for transfers between devices  771 us (78%)
  blocking collectives  134 us (14%)
  matrix products  25 us (3%)
  local copies, waits for them, and re-layouts  22.6 us (2%)
  between operations  17.5 us (2%)
  starting transfers between devices  13.3 us (1%)
    all_gather x1, waiting for transfers between devices, local(): lax.all_gather(reference_hidden, DP_VOCAB, axis=0, tiled=True)  675 us
    all_gather x5, blocking collectives, all_in_one(): both, at, found = (lax.all_gather(jnp.concatenate(lines), axis), 0, {})  103 us
    all_gather x1, waiting for transfers between devices, local(): segment = lax.all_gather(logit_grad, DP, axis=0, tiled=True)  50.3 us
    all_to_all x1, waiting for transfers between devices, sum_at_owner(): tiles = lax.all_to_all(in_blocks(value, dim, peers), axis, 0, 0, tiled=True)  44.1 us
    all_to_all x1, blocking collectives, local(): lax.all_to_all(policy_hidden, DP, split_axis=1, concat_axis=0, tiled=True)  30.3 us
  transfers between devices with their start and end apart: 4, of which 3 were waited for; matrix products, arithmetic and copies ran while one was open for 4% of the time, Pallas kernels for 0%

commit v1 on v0

--- a/solution.py
+++ b/solution.py
@@ -10,6 +10,11 @@
 DP_VOCAB = ("dp_0", "dp_1", "vocab_0", "vocab_1", "vocab_2")
 beta = 0.1
 loss_scale = 4096.0
+
+
+def all_by_exchange(value, axis, dim):
+    sent = jnp.stack([value] * lax.axis_size(axis))
+    return jnp.concatenate(lax.all_to_all(sent, axis, 0, 0), axis=dim)
 
 
 def all_in_one(value, axis):
@@ -142,7 +147,7 @@
     logit_grad = (
         token_scale[None, :] * (onehot - jnp.exp(policy_logits - policy_total[None, :]))
     ).astype(jnp.bfloat16)
-    segment = lax.all_gather(logit_grad, DP, axis=0, tiled=True)
+    segment = all_by_exchange(logit_grad, DP, 0)
     weight_block = policy_weight
     column_grad = lax.dot_general(
         columns, segment, (((0,), (1,)), ((), ())), preferred_element_type=jnp.float32

time: 991 us -> 1050 us (1.060)
  blocking collectives: 134 us -> 230 us
  waiting for transfers between devices: 771 us -> 718 us
  local copies, waits for them, and re-layouts: 22.6 us -> 37.1 us
    all_to_all x0 -> x1, blocking collectives: none -> 96.7 us  [all_by_exchange(): return jnp.concatenate(lax.all_to_all(sent, axis, 0, 0), axis=dim)]
    all_gather x1 -> x0, waiting for transfers between devices: 50.3 us -> none  [local(): segment = lax.all_gather(logit_grad, DP, axis=0, tiled=True)]
  transfers between devices with their start and end apart: 4 -> 3, of which waited for: 3 -> 2; matrix products, arithmetic and copies ran while one was open for 4% -> 4% of each run, Pallas kernels for 0% -> 0%
where the time goes in v1:
time: 1050 us
  waiting for transfers between devices  718 us (68%)
  blocking collectives  230 us (22%)
  local copies, waits for them, and re-layouts  37.1 us (4%)
  matrix products  25 us (2%)
  between operations  17.5 us (2%)
    all_gather x1, waiting for transfers between devices, local(): lax.all_gather(reference_hidden, DP_VOCAB, axis=0, tiled=True)  675 us
    all_gather x5, blocking collectives, all_in_one(): both, at, found = (lax.all_gather(jnp.concatenate(lines), axis), 0, {})  103 us
    all_to_all x1, blocking collectives, all_by_exchange(): return jnp.concatenate(lax.all_to_all(sent, axis, 0, 0), axis=dim)  96.7 us
    all_to_all x1, waiting for transfers between devices, sum_at_owner(): tiles = lax.all_to_all(in_blocks(value, dim, peers), axis, 0, 0, tiled=True)  41.5 us
    all_to_all x1, blocking collectives, local(): lax.all_to_all(policy_hidden, DP, split_axis=1, concat_axis=0, tiled=True)  30.3 us
  transfers between devices with their start and end apart: 3, of which 2 were waited for; matrix products, arithmetic and copies ran while one was open for 4% of the time, Pallas kernels for 0%

profile of v1, /device:TPU:38, one launch (start us, length us, event | category | flops | bytes accessed | tf_op | source)
XLA Modules:
  0.0 1045.2 jit_solution(8980811187186283858)
XLA Ops:
  8.1 0.7 all-gather.13.cloned.1.call-update
  8.8 2.3 copy.28
  11.1 30.3 %all_to_all.29 = bf16[128,8,512]{0,2,1:T(8,128)(2,1)S(1)} all-to-all(bf16[128,8,512]{0,2,1:T(8,128)(2,1)} %bitcast.461), channel_id=1, replica_groups=mesh['dp_0'=4,'dp_1'=2,'vocab_0'=2,'vocab_1'=4,'vocab_2'=4] {'dp_0','dp_1'}, dimensions={1} | all-to-all | bytes 2097152 | tf_op jit(solution)/shard_map/all_to_all | solution.py:107
  41.3 1.3 copy.29
  42.6 6.9 fusion.96
  49.5 0.6 copy-done.5
  50.4 675.5 %all-gather.13.cloned.1.call-done = bf16[256,4,4096]{2,1,0:T(4,128)(2,1)} async-done(((bf16[1,4,4096]{2,1,0:T(4,128)(2,1)}), bf16[256,4,4096]{2,1,0:T(4,128)(2,1)}) %all-gather.13.cloned.1.call-update) | async-done | bytes 8388624 | tf_op jit(solution)/shard_map/all_gather | solution.py:109
  725.9 12.5 %reshape.1604 = bf16[1024,4096]{1,0:T(8,128)(2,1)} reshape(bf16[256,4,4096]{2,1,0:T(4,128)(2,1)} %all-gather.13.cloned.1.call-done) | data formatting | bytes 16777216
  738.4 6.4 fusion.95
  744.8 0.3 select_reduce_fusion
  745.1 1.4 reduce_max.18
  746.5 1.5 select_reduce_fusion.1
  748.1 59.3 %all-gather.6 = f32[4,6,1024]{2,1,0:T(8,128)S(1)} all-gather(f32[1,6,1024]{2,1,0:T(8,128)S(1)} %bitcast.464), channel_id=2, replica_groups=mesh['dp_0'=4,'dp_1'=2,'vocab_0'=2,'vocab_1'=4,'vocab_2'=4] {'dp_0'}, dimensions={0}, use_global_device_ids=true | all-gather | bytes 122880 | tf_op jit(solution)/shard_map/all_gather | solution.py:28
  807.6 1.9 all-gather.7
  809.5 8.5 all-gather.8
  818.1 21.7 %all-gather.9 = f32[4,6,1024]{2,1,0:T(8,128)S(1)} all-gather(f32[1,6,1024]{2,1,0:T(8,128)S(1)} %bitcast.467), channel_id=5, replica_groups=mesh['dp_0'=4,'dp_1'=2,'vocab_0'=2,'vocab_1'=4,'vocab_2'=4] {'vocab_1'}, dimensions={0}, use_global_device_ids=true | all-gather | bytes 122880 | tf_op jit(solution)/shard_map/all_gather | solution.py:28
  840.0 12.1 %all-gather.10 = f32[4,6,1024]{2,1,0:T(8,128)S(1)} all-gather(f32[1,6,1024]{2,1,0:T(8,128)S(1)} %bitcast.468), channel_id=6, replica_groups=mesh['dp_0'=4,'dp_1'=2,'vocab_0'=2,'vocab_1'=4,'vocab_2'=4] {'vocab_2'}, dimensions={0}, use_global_device_ids=true | all-gather | bytes 122880 | tf_op jit(solution)/shard_map/all_gather | solution.py:28
  852.4 0.7 gather_fusion.1
  853.1 0.7 gather_fusion
  853.8 0.6 fusion.85
  854.6 1.1 multiply_convert_fusion
  855.7 1.2 copy.30
  857.0 0.3 stack.2
  857.2 96.7 %all_to_all.30 = bf16[8,256,1024]{1,2,0:T(8,128)(2,1)} all-to-all(bf16[8,256,1024]{1,2,0:T(8,128)(2,1)S(1)} %stack.2), channel_id=1, replica_groups=mesh['dp_0'=4,'dp_1'=2,'vocab_0'=2,'vocab_1'=4,'vocab_2'=4] {'dp_0','dp_1'}, dimensions={0} | all-to-all | bytes 8388608 | tf_op jit(solution)/shard_map/all_to_all | solution.py:17
  954.0 6.4 copy.31
  960.4 6.5 copy.32
  966.9 5.9 fusion.1
  972.9 9.4 all-to-all-start.2
  982.9 5.9 fusion
  988.8 3.9 copy.33
  992.7 41.5 %all-to-all-done.2 = f32[32,32,512]{2,1,0:T(8,128)} async-done(((f32[32,32,512]{2,1,0:T(8,128)}), f32[32,32,512]{2,1,0:T(8,128)}, u32[]{:S(2)}, u32[]{:S(2)}) %all-to-all-start.2) | async-done | bytes 2097184 | tf_op jit(solution)/shard_map/all_to_all | solution.py:54
  1034.2 2.4 reduce_sum.78
  (44 shorter events, 1.6 us)
Async XLA Ops:
  8.0 34.6 %copy-start = (bf16[512,2048]{1,0:T(8,128)(2,1)S(1)}, bf16[512,2048]{1,0:T(8,128)(2,1)}, u32[]{:S(2)}) copy-start(bf16[512,2048]{1,0:T(8,128)(2,1)} %param.8) | copy-start | bytes 6291460
  8.0 717.9 %all-gather.13.cloned.1.call-start = ((), (), s32[]{:S(2)}) async-start(), calls=%async_computation.5 | async-start | bytes 8421376 | tf_op jit(solution)/shard_map/all_gather | solution.py:109
  8.7 736.4 %reduce-scatter.2.cloned.1.call-start = ((), (), s32[]{:S(2)}) async-start(), calls=%async_computation.4 | async-start | bytes 9437184 | tf_op jit(solution)/shard_map/reduce_scatter | solution.py:118
  49.5 0.7 copy-start.5
  49.5 0.9 copy-start.4
  744.8 107.4 %copy-start.3 = (s32[1024]{0:T(1024)S(1)}, s32[1024]{0:T(1024)}, u32[]{:S(2)}) copy-start(s32[1024]{0:T(1024)} %param.12) | copy-start | bytes 12292
  745.1 109.5 %copy-start.1 = (f32[256,1024]{1,0:T(8,128)S(1)}, f32[256,1024]{1,0:T(8,128)}, u32[]{:S(2)}) copy-start(f32[256,1024]{1,0:T(8,128)} %reduce-scatter.2.cloned.1.call-done) | copy-start | bytes 3145732
  972.9 10.0 copy-start.2
  972.9 61.4 %all-to-all-start.2 = ((f32[32,32,512]{2,1,0:T(8,128)}), f32[32,32,512]{2,1,0:T(8,128)}, u32[]{:S(2)}, u32[]{:S(2)}) async-start(f32[32,32,512]{2,1,0:T(8,128)} %fusion.1), calls=%async_computation.3 | async-start | bytes 4194304 | tf_op jit(solution)/shard_map/all_to_all | solution.py:54
Sparse Core Ops, SparseCore 0:
  10.7 715.1 all-gather.12
Sparse Core Ops, SparseCore 1:
  49.6 93.9 reduce-scatter.1
